TPU v7x, 32 devices: a whole 2x2x4 slice. The times are simulated.
32 devices in a mesh: row: 4 (over x, core), col: 8 (over z, y).
Axes of the slice: x: 2, y: 2, z: 4, core: 2. Of those that a mesh axis runs over, the one named last changes fastest.
Arguments:
- matrix: float32 [2048, 8192], P('col', 'row'), may hold values from -6 to 6
- basis: float32 [8192, 512], P(('row', 'col')), may hold values from -0.0625 to 0.0625
Outputs:
- root: float32 [512, 512], P('row', 'col')
- right: float32 [2048, 512], P('col')
All inputs are finite; a program needn't handle non-finite values.
Results may differ from a plain program's by a relative error of at most 0.00018.
Values sent between devices are 32-bit elements; how exact they have to be, the bound alone decides.
A program may use at most 64 MiB of HBM per device.

v0:
```python
import jax
import jax.numpy as jnp
from jax import lax
from jax.sharding import PartitionSpec as P

ITERS = 8


def polar_steps(gram, width):
    highest = lax.Precision.HIGHEST
    scale = jnp.sqrt(jnp.sum(gram * gram) + 1e-06)
    ident = jnp.eye(width, dtype=jnp.float32)
    upper = gram / scale
    lower = ident
    for step in range(ITERS):
        middle = 0.5 * (3.0 * ident - jnp.dot(lower, upper, precision=highest))
        upper = jnp.dot(upper, middle, precision=highest)
        lower = jnp.dot(middle, lower, precision=highest)
    return (upper, lower, jnp.sqrt(scale))


def local(matrix, basis):
    highest = lax.Precision.HIGHEST
    width = basis.shape[1]
    nrow = lax.axis_size("row")
    ncol = lax.axis_size("col")
    partial_proj = lax.dot_general(
        lax.all_gather(basis, "col", axis=0, tiled=True),
        matrix,
        (((0,), (1,)), ((), ())),
        precision=highest,
    )
    proj = lax.psum(partial_proj, "row")
    gram = lax.psum(jnp.dot(proj, proj.T, precision=highest), "col")
    upper, lower, root_scale = polar_steps(gram, width)
    right = jnp.dot(proj.T, lower, precision=highest) / root_scale
    root_full = upper * root_scale
    row_len = width // nrow
    col_len = width // ncol
    root = lax.dynamic_slice(
        root_full,
        (lax.axis_index("row") * row_len, lax.axis_index("col") * col_len),
        (row_len, col_len),
    )
    return (root, right)


def solution(mesh):
    return jax.shard_map(
        local,
        mesh=mesh,
        in_specs=(P("col", "row"), P(("row", "col"), None)),
        out_specs=(P("row", "col"), P("col", None)),
        check_vma=False,
    )
```

profile of v0, /device:TPU:0, one launch (start us, length us, event | category | flops | bytes accessed | tf_op | source)
XLA Modules:
  0.0 268.9 jit_solution(109907291531495080)
XLA Ops:
  8.0 77.7 %all-gather.2.cloned.1.call-done = f32[2048,512]{1,0:T(8,128)} async-done(((f32[256,512]{1,0:T(8,128)}), f32[2048,512]{1,0:T(8,128)}) %all-gather.2.cloned.1.call-update) | async-done | bytes 4194320 | tf_op jit(solution)/shard_map/all_gather | solution.py:28
  85.7 9.6 %fusion.10 = f32[512,256]{1,0:T(8,128)} fusion(f32[2048,512]{1,0:T(8,128)} %all-gather.2.cloned.1.call-done, f32[256,2048]{1,0:T(8,128)S(1)} %copy-done), kind=kOutput, calls=%fused_computation.23 | convolution fusion | flops 3221225472 | bytes 6815744 | tf_op jit(solution)/shard_map/dot_general | solution.py:27
  95.5 31.9 %all-reduce.3.cloned.1.call-done = f32[512,256]{1,0:T(8,128)} async-done(((f32[512,256]{1,0:T(8,128)}), f32[512,256]{1,0:T(8,128)}) %all-reduce.3.cloned.1.call-update) | async-done | bytes 524304 | tf_op jit(solution)/shard_map/psum | solution.py:33
  127.4 3.2 %fusion.11 = f32[512,512]{1,0:T(8,128)} fusion(f32[512,256]{1,0:T(8,128)} %all-reduce.3.cloned.1.call-done), kind=kOutput, calls=%fused_computation.24 | convolution fusion | flops 805306368 | bytes 1572864 | tf_op jit(solution)/shard_map/dot_general | solution.py:34
  130.7 78.7 %all-reduce.5.cloned.1.call-done = f32[512,512]{1,0:T(8,128)} async-done(((f32[512,512]{1,0:T(8,128)}), f32[512,512]{1,0:T(8,128)}) %all-reduce.5.cloned.1.call-update) | async-done | bytes 1048592 | tf_op jit(solution)/shard_map/psum | solution.py:34
  209.4 2.2 multiply_reduce_fusion
  212.3 2.3 fusion.7
  215.6 1.9 fusion.9
  217.5 1.9 fusion
  221.2 1.8 fusion.13
  223.0 2.1 fusion.1
  225.1 1.8 fusion.15
  228.8 1.8 fusion.2
  234.4 1.9 fusion.3
  236.2 2.3 fusion.19
  238.5 1.8 fusion.18
  240.4 1.8 fusion.4
  242.2 1.8 fusion.21
  245.9 1.8 fusion.5
  249.7 3.0 %fusion.22 = f32[512,512]{1,0:T(8,128)} fusion(f32[512,512]{1,0:T(8,128)S(1)} %fusion.20, f32[512,512]{1,0:T(8,128)S(1)} %fusion.5), kind=kOutput, calls=%fused_computation.35 | convolution fusion | flops 1610612736 | bytes 3145728 | tf_op jit(solution)/shard_map/dot_general | solution.py:17
  252.7 3.2 %fusion.6 = f32[512,512]{1,0:T(8,128)S(1)} fusion(f32[512,512]{1,0:T(8,128)S(1)} %fusion.23, f32[512,512]{1,0:T(8,128)} %fusion.22), kind=kOutput, calls=%fused_computation.14 | convolution fusion | flops 1611661312 | bytes 3145728 | tf_op jit(solution)/shard_map/dot_general | solution.py:16
  255.9 1.8 fusion.25
  257.8 1.9 fusion.24
  260.3 1.9 convolution_divide_fusion
  (22 shorter events, 13.7 us)
Async XLA Ops:
  7.2 78.5 %copy-start = (f32[256,2048]{1,0:T(8,128)S(1)}, f32[256,2048]{1,0:T(8,128)}, u32[]{:S(2)}) copy-start(f32[256,2048]{1,0:T(8,128)} %param.2) | copy-start | bytes 6291460
  7.2 78.5 %all-gather.2.cloned.1.call-start = ((), (), s32[]{:S(2)}) async-start(), calls=%async_computation | async-start | bytes 4718592 | tf_op jit(solution)/shard_map/all_gather | solution.py:28
  7.9 119.5 %all-reduce.3.cloned.1.call-start = ((), (), s32[]{:S(2)}) async-start(), calls=%async_computation.1 | async-start | bytes 1048576 | tf_op jit(solution)/shard_map/psum | solution.py:33
  95.3 114.0 %all-reduce.5.cloned.1.call-start = ((), (), s32[]{:S(2)}) async-start(), calls=%async_computation.2 | async-start | bytes 2097152 | tf_op jit(solution)/shard_map/psum | solution.py:34
  209.4 6.2 %copy-start.3 = (f32[512,512]{1,0:T(8,128)S(1)}, f32[512,512]{1,0:T(8,128)}, u32[]{:S(2)}) copy-start(f32[512,512]{1,0:T(8,128)} %all-reduce.5.cloned.1.call-done) | copy-start | bytes 3145732
  252.7 5.1 %copy-start.1 = (f32[512,512]{1,0:T(8,128)S(1)}, f32[512,512]{1,0:T(8,128)}, u32[]{:S(2)}) copy-start(f32[512,512]{1,0:T(8,128)} %fusion.22) | copy-start | bytes 3145732
  252.7 7.6 %copy-start.2 = (f32[512,256]{1,0:T(8,128)S(1)}, f32[512,256]{1,0:T(8,128)}, u32[]{:S(2)}) copy-start(f32[512,256]{1,0:T(8,128)} %all-reduce.3.cloned.1.call-done) | copy-start | bytes 1572868
Sparse Core Ops, SparseCore 0:
  10.1 75.5 all-gather.1
  95.4 31.9 all-reduce.2
  130.9 78.3 all-reduce.4
where the time goes:
time: 274 us; the launch traced here: 269 us
  waiting for transfers between devices  189 us (69%)
  matrix products  61.9 us (23%)
  between operations  14.9 us (5%)
  other arithmetic  2.82 us (1%)
    psum x1, waiting for transfers between devices, local(): gram = lax.psum(jnp.dot(proj, proj.T, precision=highest), 'col')  78.7 us
    all_gather x1, waiting for transfers between devices, local(): lax.all_gather(basis, 'col', axis=0, tiled=True)  77.7 us
    psum x1, waiting for transfers between devices, local(): proj = lax.psum(partial_proj, 'row')  31.9 us
    dot_general x8, matrix products, polar_steps(): middle = 0.5 * (3.0 * ident - jnp.dot(lower, upper, precision=highest))  16.8 us
    dot_general x8, matrix products, polar_steps(): upper = jnp.dot(upper, middle, precision=highest)  16 us
    dot_general x8, matrix products, polar_steps(): lower = jnp.dot(middle, lower, precision=highest)  14.3 us
    dot_general x1, matrix products, local(): lax.dot_general(lax.all_gather(basis, 'col', axis=0, tiled=True), matrix,...  9.64 us
  transfers between devices with their start and end apart: 3, of which 3 were waited for; matrix products, arithmetic and copies ran while one was open for 0% of the time, Pallas kernels for 0%

commit v1 on v0

--- a/solution.py
+++ b/solution.py
@@ -30,7 +30,10 @@
         (((0,), (1,)), ((), ())),
         precision=highest,
     )
-    proj = lax.psum(partial_proj, "row")
+    devs = jax.lax.axis_size("row")
+    proj = partial_proj
+    for ix in [[(k, k ^ idx) for k in range(devs)] for idx in (1, 2, 4, 8, 16) if idx < devs]:
+        proj = proj + jax.lax.ppermute(proj, "row", ix)
     gram = lax.psum(jnp.dot(proj, proj.T, precision=highest), "col")
     upper, lower, root_scale = polar_steps(gram, width)
     right = jnp.dot(proj.T, lower, precision=highest) / root_scale

time: 274 us -> 254 us (0.927)
  waiting for transfers between devices: 189 us -> 170 us
    psum x1 -> x0, waiting for transfers between devices: 31.9 us -> none  [local(): proj = lax.psum(partial_proj, 'row')]
    ppermute x0 -> x2, waiting for transfers between devices: none -> 14.4 us  [local(): proj = proj + jax.lax.ppermute(proj, 'row', ix)]
  transfers between devices with their start and end apart: 3 -> 4, of which waited for: 3 -> 4; matrix products, arithmetic and copies ran while one was open for 0% -> 0% of each run, Pallas kernels for 0% -> 0%
where the time goes in v1:
time: 254 us; the launch traced here: 251 us
  waiting for transfers between devices  170 us (67%)
  matrix products  60 us (24%)
  between operations  15.3 us (6%)
  other arithmetic  2.94 us (1%)
    all_gather x1, waiting for transfers between devices, local(): lax.all_gather(basis, 'col', axis=0, tiled=True)  77.7 us
    psum x1, waiting for transfers between devices, local(): gram = lax.psum(jnp.dot(proj, proj.T, precision=highest), 'col')  77 us
    dot_general x8, matrix products, polar_steps(): middle = 0.5 * (3.0 * ident - jnp.dot(lower, upper, precision=highest))  16.8 us
    dot_general x8, matrix products, polar_steps(): upper = jnp.dot(upper, middle, precision=highest)  16.1 us
    ppermute x2, waiting for transfers between devices, local(): proj = proj + jax.lax.ppermute(proj, 'row', ix)  14.4 us
    dot_general x8, matrix products, polar_steps(): lower = jnp.dot(middle, lower, precision=highest)  14.1 us
    dot_general x1, matrix products, local(): lax.dot_general(lax.all_gather(basis, 'col', axis=0, tiled=True), matrix,...  9.07 us
  transfers between devices with their start and end apart: 4, of which 4 were waited for; matrix products, arithmetic and copies ran while one was open for 0% of the time, Pallas kernels for 0%

profile of v1, /device:TPU:0, one launch (start us, length us, event | category | flops | bytes accessed | tf_op | source)
XLA Modules:
  0.0 250.5 jit_solution(4577243097004862450)
XLA Ops:
  8.0 77.7 %all-gather.2.cloned.1.call-done = f32[2048,512]{1,0:T(8,128)} async-done(((f32[256,512]{1,0:T(8,128)}), f32[2048,512]{1,0:T(8,128)}) %all-gather.2.cloned.1.call-update) | async-done | bytes 4194320 | tf_op jit(solution)/shard_map/all_gather | solution.py:28
  85.7 9.1 %fusion.10 = f32[512,256]{1,0:T(8,128)S(1)} fusion(f32[2048,512]{1,0:T(8,128)} %all-gather.2.cloned.1.call-done, f32[256,2048]{1,0:T(8,128)S(1)} %copy-done), kind=kOutput, calls=%fused_computation.23 | convolution fusion | flops 3221225472 | bytes 6815744 | tf_op jit(solution)/shard_map/dot_general | solution.py:27
  94.8 1.9 collective-permute-done
  98.3 12.5 %collective-permute-done.1 = f32[512,256]{1,0:T(8,128)S(1)} collective-permute-done((f32[512,256]{1,0:T(8,128)S(1)}, f32[512,256]{1,0:T(8,128)S(1)}, u32[]{:S(2)}, u32[]{:S(2)}) %collective-permute-start.1) | collective-permute-done | bytes 524320 | tf_op jit(solution)/shard_map/ppermute | solution.py:36
  111.7 2.1 fusion.11
  113.8 77.0 %all-reduce.2.cloned.1.call-done = f32[512,512]{1,0:T(8,128)} async-done(((f32[512,512]{1,0:T(8,128)}), f32[512,512]{1,0:T(8,128)}) %all-reduce.2.cloned.1.call-update) | async-done | bytes 1048592 | tf_op jit(solution)/shard_map/psum | solution.py:37
  190.8 2.2 multiply_reduce_fusion
  193.7 2.3 fusion.7
  197.0 1.9 fusion.9
  198.9 1.8 fusion
  204.4 2.0 fusion.1
  206.5 1.8 fusion.15
  210.2 1.9 fusion.2
  213.9 1.8 fusion.16
  215.8 1.8 fusion.3
  217.6 2.1 fusion.19
  219.7 1.8 fusion.18
  221.6 1.9 fusion.4
  223.4 1.8 fusion.21
  227.1 1.8 fusion.5
  230.8 3.1 %fusion.22 = f32[512,512]{1,0:T(8,128)} fusion(f32[512,512]{1,0:T(8,128)S(1)} %fusion.20, f32[512,512]{1,0:T(8,128)S(1)} %fusion.5), kind=kOutput, calls=%fused_computation.35 | convolution fusion | flops 1610612736 | bytes 3145728 | tf_op jit(solution)/shard_map/dot_general | solution.py:17
  234.0 3.2 %fusion.6 = f32[512,512]{1,0:T(8,128)S(1)} fusion(f32[512,512]{1,0:T(8,128)S(1)} %fusion.23, f32[512,512]{1,0:T(8,128)} %fusion.22), kind=kOutput, calls=%fused_computation.14 | convolution fusion | flops 1611661312 | bytes 3145728 | tf_op jit(solution)/shard_map/dot_general | solution.py:16
  239.1 1.9 fusion.24
  241.0 1.9 convolution_divide_fusion
  (27 shorter events, 17.9 us)
Async XLA Ops:
  7.2 78.5 %copy-start = (f32[256,2048]{1,0:T(8,128)S(1)}, f32[256,2048]{1,0:T(8,128)}, u32[]{:S(2)}) copy-start(f32[256,2048]{1,0:T(8,128)} %param.2) | copy-start | bytes 6291460
  7.2 78.5 %all-gather.2.cloned.1.call-start = ((), (), s32[]{:S(2)}) async-start(), calls=%async_computation | async-start | bytes 4718592 | tf_op jit(solution)/shard_map/all_gather | solution.py:28
  7.9 182.9 %all-reduce.2.cloned.1.call-start = ((), (), s32[]{:S(2)}) async-start(), calls=%async_computation.1 | async-start | bytes 2097152 | tf_op jit(solution)/shard_map/psum | solution.py:37
  94.7 2.0 collective-permute-start
  96.8 14.0 %collective-permute-start.1 = (f32[512,256]{1,0:T(8,128)S(1)}, f32[512,256]{1,0:T(8,128)S(1)}, u32[]{:S(2)}, u32[]{:S(2)}) collective-permute-start(f32[512,256]{1,0:T(8,128)S(1)} %add.17), channel_id=1, source_target_pairs={{0,16},{8,24},{16,0},{24,8},{1,17},{9,25},{17,1},{25,9},{2,18},{10... | collective-permute-start | bytes 1572872 | tf_op jit(solution)/shard_map/ppermute | solution.py:36
  110.9 0.8 copy-start.2
  190.8 6.2 %copy-start.4 = (f32[512,512]{1,0:T(8,128)S(1)}, f32[512,512]{1,0:T(8,128)}, u32[]{:S(2)}) copy-start(f32[512,512]{1,0:T(8,128)} %all-reduce.2.cloned.1.call-done) | copy-start | bytes 3145732
  234.0 5.1 %copy-start.1 = (f32[512,512]{1,0:T(8,128)S(1)}, f32[512,512]{1,0:T(8,128)}, u32[]{:S(2)}) copy-start(f32[512,512]{1,0:T(8,128)} %fusion.22) | copy-start | bytes 3145732
  234.0 7.0 %copy-start.3 = (f32[512,256]{1,0:T(8,128)S(1)}, f32[512,256]{1,0:T(8,128)}, u32[]{:S(2)}) copy-start(f32[512,256]{1,0:T(8,128)} %copy-done.2) | copy-start | bytes 1572868
Sparse Core Ops, SparseCore 0:
  10.1 75.5 all-gather.1
  113.9 76.8 all-reduce.1
